TPU v7x, 256 devices: a whole 4x4x8 slice. The times are simulated.
256 devices in a mesh: row: 16 (over z, core), col: 16 (over y, x).
Axes of the slice: x: 4, y: 4, z: 8, core: 2. Of those that a mesh axis runs over, the one named last changes fastest.
Arguments:
- design: float32 [8192, 65536], P('row', 'col'), may hold values from -0.0625 to 0.0625
- targets: float32 [32, 8192], P(None, 'row'), may hold values from -6 to 6
- warm_solution: float32 [32, 65536], P(None, ('col', 'row')), may hold values from -2 to 2
- warm_sparse: float32 [32, 65536], P(None, ('col', 'row')), may hold values from -2 to 2
- warm_dual: float32 [32, 65536], P(None, ('col', 'row')), may hold values from -1.5 to 1.5
- sparsity: float32 [32], replicated, may hold values from 0.02 to 0.2
Outputs:
- solution: float32 [32, 65536], P(None, ('col', 'row'))
- sparse: float32 [32, 65536], P(None, ('col', 'row'))
- scaled_dual: float32 [32, 65536], P(None, ('col', 'row'))
All inputs are finite; a program needn't handle non-finite values.
Results may differ from a plain program's by a relative error of at most 0.0003.
Values sent between devices are 32-bit elements; how exact they have to be, the bound alone decides.
No kernel may reach another device: no remote copies, remote signals or barrier semaphores. Data moves between devices by JAX's collectives and lax.ppermute only.
A program may use at most 64 MiB of HBM per device.

v0:
```python
import jax
import jax.numpy as jnp
from jax import lax
from jax.sharding import Mesh
from jax.sharding import PartitionSpec as P

STEPS = 3
COL = ("col_0", "col_1")
ROW = ("row_0", "row_1")
ROW_COL = ("row_0", "row_1", "col_0", "col_1")
COL_ROW = ("col_0", "col_1", "row_0", "row_1")
penalty = 0.5


def sent_to_all(array, axis):
    peers = lax.axis_size(axis)
    return lax.all_to_all(
        jnp.broadcast_to(array[None], (peers, *array.shape)), axis, 0, 0, tiled=True
    )


def taken_together(array, axis):
    everything = sent_to_all(array, axis)
    return jnp.sum(everything, axis=0)


def split_up(array, dim, peers):
    before, after = (array.shape[:dim], array.shape[dim + 1 :])
    return jnp.moveaxis(array.reshape(*before, peers, -1, *after), dim, 0)


def summed_on_arrival(array, axis, dim):
    peers = lax.axis_size(axis)
    tiles = lax.all_to_all(split_up(array, dim, peers), axis, 0, 0, tiled=True)
    return jnp.sum(tiles, axis=0)


def by_axis(array, axes):
    for axis in axes:
        array = lax.psum(array, axis)
    return array


def forward_part(vector, block):
    return lax.dot_general(
        vector,
        block,
        (((1,), (1,)), ((), ())),
        precision=lax.Precision.HIGHEST,
        preferred_element_type=jnp.float32,
    )


def backward_part(values, design):
    return jnp.dot(
        values, design, precision=lax.Precision.HIGHEST, preferred_element_type=jnp.float32
    )


def row_sums(values):
    return jnp.sum(values, axis=1, keepdims=True)


def on_device(design, targets, warm_solution, warm_sparse, warm_dual, sparsity):

    def rows_total(partial_value):
        return taken_together(partial_value, COL)

    def spread(vector):
        return rows_total(forward_part(lax.all_gather(vector, ROW, axis=1, tiled=True), design))

    def collect(values):
        return summed_on_arrival(backward_part(values, design), ROW, 1)

    def total(stats):
        return jax.tree.map(lambda part: by_axis(part, ROW_COL), stats)

    solution, sparse, scaled_dual = (warm_solution, warm_sparse, warm_dual)

    def gram(vector):
        return collect(spread(vector)) + penalty * vector

    thresh = (sparsity / penalty)[:, None]
    residual = collect(targets - spread(solution)) + penalty * (sparse - scaled_dual - solution)
    image = gram(residual)
    norm_now, product = total((row_sums(residual * residual), row_sums(residual * image)))
    alpha = norm_now / product
    direction = residual
    along = image
    for step in range(STEPS):
        solution = solution + alpha * direction
        residual = residual - alpha * along
        if step + 1 < STEPS:
            image = gram(residual)
            norm_next, product = total((row_sums(residual * residual), row_sums(residual * image)))
            ratio = norm_next / norm_now
            alpha = norm_next / (product - ratio * norm_next / alpha)
            direction = residual + ratio * direction
            along = image + ratio * along
            norm_now = norm_next
    merged = solution + scaled_dual
    sparse = jnp.sign(merged) * jnp.maximum(jnp.abs(merged) - thresh, 0.0)
    scaled_dual = merged - sparse
    return (solution, sparse, scaled_dual)


def solution(mesh):
    finer = Mesh(mesh.devices.reshape(8, 2, 4, 4), ("row_0", "row_1", "col_0", "col_1"))
    return jax.shard_map(
        on_device,
        mesh=finer,
        in_specs=(
            P(ROW, COL),
            P(None, ROW),
            P(None, COL_ROW),
            P(None, COL_ROW),
            P(None, COL_ROW),
            P(),
        ),
        out_specs=(P(None, COL_ROW), P(None, COL_ROW), P(None, COL_ROW)),
        check_vma=False,
    )
```

profile of v0, /device:TPU:2, one launch (start us, length us, event | category | flops | bytes accessed | tf_op | source)
XLA Modules:
  0.0 428.4 jit_solution(11205787050152184294)
XLA Ops:
  0.6 21.7 %all_gather.12 = f32[32,4096]{1,0:T(8,128)S(1)} all-gather(f32[32,256]{1,0:T(8,128)} %param.8), channel_id=1, replica_groups=mesh['row_0'=8,'row_1'=2,'col_0'=4,'col_1'=4] {'row_0','row_1'}, dimensions={1}, use_global_device_ids=true | all-gather | bytes 557056 | tf_op jit(solution)/shard_map/all_gather | solution.py:70
  22.3 9.7 %fusion.8 = f32[32,512]{1,0:T(8,128)S(1)} fusion(f32[32,4096]{1,0:T(8,128)S(1)} %all_gather.12, f32[512,4096]{1,0:T(8,128)} %param.6), kind=kOutput, calls=%fused_computation.30 | convolution fusion | flops 805306368 | bytes 8978432 | tf_op jit(solution)/shard_map/dot_general | solution.py:45
  32.2 23.6 %all_to_all.40 = f32[16,32,512]{2,1,0:T(8,128)S(1)} all-to-all(f32[16,32,512]{2,1,0:T(8,128)S(1)} %broadcast_in_dim.20), channel_id=1, replica_groups=mesh['row_0'=8,'row_1'=2,'col_0'=4,'col_1'=4] {'col_0','col_1'}, dimensions={0} | all-to-all | bytes 2097152 | tf_op jit(solution)/shard_map/all_to_all | solution.py:17
  55.9 7.2 %fusion.3 = f32[32,4096]{1,0:T(8,128)S(1)} fusion(f32[512,4096]{1,0:T(8,128)} %param.6, f32[32,512]{1,0:T(8,128)S(1)} %copy-done.2, f32[32,512]{1,0:T(8,128)S(1)} %reduce_sum.126), kind=kOutput, calls=%fused_computation.7 | convolution fusion | flops 805322752 | bytes 9043968 | tf_op jit(solution)/shard_map/dot_general | solution.py:55
  63.1 19.5 %all_to_all.41 = f32[16,32,256]{2,1,0:T(8,128)S(1)} all-to-all(f32[16,32,256]{2,1,0:T(8,128)S(1)} %bitcast.55), channel_id=1, replica_groups=mesh['row_0'=8,'row_1'=2,'col_0'=4,'col_1'=4] {'row_0','row_1'}, dimensions={0} | all-to-all | bytes 1048576 | tf_op jit(solution)/shard_map/all_to_all | solution.py:34
  82.7 17.2 %all_gather.13 = f32[32,4096]{1,0:T(8,128)S(1)} all-gather(f32[32,256]{1,0:T(8,128)S(1)} %multiply_add_fusion.3), channel_id=1, replica_groups=mesh['row_0'=8,'row_1'=2,'col_0'=4,'col_1'=4] {'row_0','row_1'}, dimensions={1}, use_global_device_ids=true | all-gather | bytes 557056 | tf_op jit(solution)/shard_map/all_gather | solution.py:70
  99.9 9.7 %fusion.9 = f32[32,512]{1,0:T(8,128)S(1)} fusion(f32[32,4096]{1,0:T(8,128)S(1)} %all_gather.13, f32[512,4096]{1,0:T(8,128)} %param.6), kind=kOutput, calls=%fused_computation.31 | convolution fusion | flops 805306368 | bytes 8978432 | tf_op jit(solution)/shard_map/dot_general | solution.py:45
  110.8 4.9 %all-to-all-start.2 = ((f32[16,32,512]{2,1,0:T(8,128)}), f32[16,32,512]{2,1,0:T(8,128)S(1)}, u32[]{:S(2)}, u32[]{:S(2)}) async-start(f32[16,32,512]{2,1,0:T(8,128)} %broadcast_in_dim.22), calls=%async_computation.2 | async-start | bytes 2097152 | tf_op jit(solution)/shard_map/all_to_all | solution.py:17
  115.7 9.0 %copy.20 = f32[4096,512]{1,0:T(8,128)} copy(f32[4096,512]{0,1:T(8,128)} %bitcast.50) | data formatting | bytes 16777216 | tf_op jit(solution)/shard_map/dot_general | solution.py:55
  124.7 7.7 %all-to-all-done.2 = f32[16,32,512]{2,1,0:T(8,128)S(1)} async-done(((f32[16,32,512]{2,1,0:T(8,128)}), f32[16,32,512]{2,1,0:T(8,128)S(1)}, u32[]{:S(2)}, u32[]{:S(2)}) %all-to-all-start.2) | async-done | bytes 1048608 | tf_op jit(solution)/shard_map/all_to_all | solution.py:17
  132.5 9.9 %convolution_bitcast_fusion.2 = f32[16,32,256]{2,1,0:T(8,128)S(1)} fusion(f32[16,256,512]{2,1,0:T(8,128)} %bitcast.51, f32[32,512]{1,0:T(8,128)S(1)} %reduce_sum.129), kind=kOutput, calls=%fused_computation.2 | convolution fusion | flops 805306368 | bytes 8978432 | tf_op jit(solution)/shard_map/dot_general | solution.py:55
  142.4 20.9 %all_to_all.42 = f32[16,32,256]{2,1,0:T(8,128)S(1)} all-to-all(f32[16,32,256]{2,1,0:T(8,128)S(1)} %convolution_bitcast_fusion.2), channel_id=1, replica_groups=mesh['row_0'=8,'row_1'=2,'col_0'=4,'col_1'=4] {'row_0','row_1'}, dimensions={0} | all-to-all | bytes 1048576 | tf_op jit(solution)/shard_map/all_to_all | solution.py:34
  163.4 14.9 %all-reduce.2 = (f32[32,1]{0,1:T(1,128)S(1)}, f32[32,1]{0,1:T(1,128)S(1)}) all-reduce(f32[32,1]{0,1:T(1,128)S(1)} %bitcast.62, f32[32,1]{0,1:T(1,128)S(1)} %bitcast.61), channel_id=1, replica_groups=mesh['row_0'=8,'row_1'=2,'col_0'=4,'col_1'=4] {'row_0'}, use_global_device_ids=true, to_apply=%region_3.0 | all-reduce | flops 64 | bytes 512 | tf_op jit(solution)/shard_map/psum | solution.py:40
  180.7 9.1 %all-reduce.8 = (f32[32,1]{0,1:T(1,128)S(1)}, f32[32,1]{0,1:T(1,128)S(1)}) all-reduce(f32[32,1]{0,1:T(1,128)S(1)} %get-tuple-element.31, f32[32,1]{0,1:T(1,128)S(1)} %get-tuple-element.32), channel_id=1, replica_groups=mesh['row_0'=8,'row_1'=2,'col_0'=4,'col_1'=4] {'col_0'}, use_global_device_ids=true, to_apply=%region_5.0 | all-reduce | flops 64 | bytes 512 | tf_op jit(solution)/shard_map/psum | solution.py:40
  189.8 10.1 %all-reduce.5 = (f32[32,1]{0,1:T(1,128)S(1)}, f32[32,1]{0,1:T(1,128)S(1)}) all-reduce(f32[32,1]{0,1:T(1,128)S(1)} %get-tuple-element.25, f32[32,1]{0,1:T(1,128)S(1)} %get-tuple-element.26), channel_id=1, replica_groups=mesh['row_0'=8,'row_1'=2,'col_0'=4,'col_1'=4] {'col_1'}, use_global_device_ids=true, to_apply=%region_6.0 | all-reduce | flops 64 | bytes 512 | tf_op jit(solution)/shard_map/psum | solution.py:40
  200.0 16.8 %all_gather.14 = f32[32,4096]{1,0:T(8,128)S(1)} all-gather(f32[32,256]{1,0:T(8,128)S(1)} %multiply_subtract_fusion.1), channel_id=1, replica_groups=mesh['row_0'=8,'row_1'=2,'col_0'=4,'col_1'=4] {'row_0','row_1'}, dimensions={1}, use_global_device_ids=true | all-gather | bytes 557056 | tf_op jit(solution)/shard_map/all_gather | solution.py:70
  216.9 9.7 %fusion.10 = f32[32,512]{1,0:T(8,128)S(1)} fusion(f32[32,4096]{1,0:T(8,128)S(1)} %all_gather.14, f32[512,4096]{1,0:T(8,128)} %param.6), kind=kOutput, calls=%fused_computation.32 | convolution fusion | flops 805306368 | bytes 8978432 | tf_op jit(solution)/shard_map/dot_general | solution.py:45
  226.7 19.7 %all_to_all.43 = f32[16,32,512]{2,1,0:T(8,128)S(1)} all-to-all(f32[16,32,512]{2,1,0:T(8,128)S(1)} %broadcast_in_dim.48), channel_id=1, replica_groups=mesh['row_0'=8,'row_1'=2,'col_0'=4,'col_1'=4] {'col_0','col_1'}, dimensions={0} | all-to-all | bytes 2097152 | tf_op jit(solution)/shard_map/all_to_all | solution.py:17
  246.5 9.9 %convolution_bitcast_fusion.1 = f32[16,32,256]{2,1,0:T(8,128)S(1)} fusion(f32[16,256,512]{2,1,0:T(8,128)} %bitcast.52, f32[32,512]{1,0:T(8,128)S(1)} %reduce_sum.133), kind=kOutput, calls=%fused_computation.1 | convolution fusion | flops 805306368 | bytes 8978432 | tf_op jit(solution)/shard_map/dot_general | solution.py:55
  256.4 21.1 %all_to_all.44 = f32[16,32,256]{2,1,0:T(8,128)S(1)} all-to-all(f32[16,32,256]{2,1,0:T(8,128)S(1)} %convolution_bitcast_fusion.1), channel_id=1, replica_groups=mesh['row_0'=8,'row_1'=2,'col_0'=4,'col_1'=4] {'row_0','row_1'}, dimensions={0} | all-to-all | bytes 1048576 | tf_op jit(solution)/shard_map/all_to_all | solution.py:34
  277.7 14.9 %all-reduce.1 = (f32[32,1]{0,1:T(1,128)S(1)}, f32[32,1]{0,1:T(1,128)S(1)}) all-reduce(f32[32,1]{0,1:T(1,128)S(1)} %bitcast.64, f32[32,1]{0,1:T(1,128)S(1)} %bitcast.63), channel_id=1, replica_groups=mesh['row_0'=8,'row_1'=2,'col_0'=4,'col_1'=4] {'row_0'}, use_global_device_ids=true, to_apply=%region_15.0 | all-reduce | flops 64 | bytes 512 | tf_op jit(solution)/shard_map/psum | solution.py:40
  295.0 8.6 %all-reduce.7 = (f32[32,1]{0,1:T(1,128)S(1)}, f32[32,1]{0,1:T(1,128)S(1)}) all-reduce(f32[32,1]{0,1:T(1,128)S(1)} %get-tuple-element.29, f32[32,1]{0,1:T(1,128)S(1)} %get-tuple-element.30), channel_id=1, replica_groups=mesh['row_0'=8,'row_1'=2,'col_0'=4,'col_1'=4] {'col_0'}, use_global_device_ids=true, to_apply=%region_17.0 | all-reduce | flops 64 | bytes 512 | tf_op jit(solution)/shard_map/psum | solution.py:40
  303.6 9.1 %all-reduce.4 = (f32[32,1]{0,1:T(1,128)S(1)}, f32[32,1]{0,1:T(1,128)S(1)}) all-reduce(f32[32,1]{0,1:T(1,128)S(1)} %get-tuple-element.23, f32[32,1]{0,1:T(1,128)S(1)} %get-tuple-element.24), channel_id=1, replica_groups=mesh['row_0'=8,'row_1'=2,'col_0'=4,'col_1'=4] {'col_1'}, use_global_device_ids=true, to_apply=%region_18.0 | all-reduce | flops 64 | bytes 512 | tf_op jit(solution)/shard_map/psum | solution.py:40
  312.8 17.0 %all_gather.15 = f32[32,4096]{1,0:T(8,128)S(1)} all-gather(f32[32,256]{1,0:T(8,128)S(1)} %multiply_subtract_fusion), channel_id=1, replica_groups=mesh['row_0'=8,'row_1'=2,'col_0'=4,'col_1'=4] {'row_0','row_1'}, dimensions={1}, use_global_device_ids=true | all-gather | bytes 557056 | tf_op jit(solution)/shard_map/all_gather | solution.py:70
  329.8 9.7 %fusion.11 = f32[32,512]{1,0:T(8,128)S(1)} fusion(f32[32,4096]{1,0:T(8,128)S(1)} %all_gather.15, f32[512,4096]{1,0:T(8,128)} %param.6), kind=kOutput, calls=%fused_computation.33 | convolution fusion | flops 805306368 | bytes 8978432 | tf_op jit(solution)/shard_map/dot_general | solution.py:45
  339.7 20.1 %all_to_all.45 = f32[16,32,512]{2,1,0:T(8,128)S(1)} all-to-all(f32[16,32,512]{2,1,0:T(8,128)S(1)} %broadcast_in_dim.51), channel_id=1, replica_groups=mesh['row_0'=8,'row_1'=2,'col_0'=4,'col_1'=4] {'col_0','col_1'}, dimensions={0} | all-to-all | bytes 2097152 | tf_op jit(solution)/shard_map/all_to_all | solution.py:17
  359.8 10.7 %convolution_bitcast_fusion = f32[16,32,256]{2,1,0:T(8,128)} fusion(f32[16,256,512]{2,1,0:T(8,128)} %bitcast.53, f32[32,512]{1,0:T(8,128)S(1)} %reduce_sum.137), kind=kOutput, calls=%fused_computation | convolution fusion | flops 805306368 | bytes 8978432 | tf_op jit(solution)/shard_map/dot_general | solution.py:55
  370.5 5.3 %all-to-all-start.7 = ((f32[16,32,256]{2,1,0:T(8,128)}), f32[16,32,256]{2,1,0:T(8,128)S(1)}, u32[]{:S(2)}, u32[]{:S(2)}) async-start(f32[16,32,256]{2,1,0:T(8,128)} %convolution_bitcast_fusion), calls=%async_computation.7 | async-start | bytes 1048576 | tf_op jit(solution)/shard_map/all_to_all | solution.py:34
  375.9 15.9 %all-to-all-done.7 = f32[16,32,256]{2,1,0:T(8,128)S(1)} async-done(((f32[16,32,256]{2,1,0:T(8,128)}), f32[16,32,256]{2,1,0:T(8,128)S(1)}, u32[]{:S(2)}, u32[]{:S(2)}) %all-to-all-start.7) | async-done | bytes 524320 | tf_op jit(solution)/shard_map/all_to_all | solution.py:34
  392.0 14.9 %all-reduce = (f32[32,1]{0,1:T(1,128)S(1)}, f32[32,1]{0,1:T(1,128)S(1)}) all-reduce(f32[32,1]{0,1:T(1,128)S(1)} %bitcast.60, f32[32,1]{0,1:T(1,128)S(1)} %bitcast.59), channel_id=1, replica_groups=mesh['row_0'=8,'row_1'=2,'col_0'=4,'col_1'=4] {'row_0'}, use_global_device_ids=true, to_apply=%region_27.0 | all-reduce | flops 64 | bytes 512 | tf_op jit(solution)/shard_map/psum | solution.py:40
  409.3 8.6 %all-reduce.6 = (f32[32,1]{0,1:T(1,128)S(1)}, f32[32,1]{0,1:T(1,128)S(1)}) all-reduce(f32[32,1]{0,1:T(1,128)S(1)} %get-tuple-element.27, f32[32,1]{0,1:T(1,128)S(1)} %get-tuple-element.28), channel_id=1, replica_groups=mesh['row_0'=8,'row_1'=2,'col_0'=4,'col_1'=4] {'col_0'}, use_global_device_ids=true, to_apply=%region_29.0 | all-reduce | flops 64 | bytes 512 | tf_op jit(solution)/shard_map/psum | solution.py:40
  417.9 9.1 %all-reduce.3 = (f32[32,1]{0,1:T(1,128)S(1)}, f32[32,1]{0,1:T(1,128)S(1)}) all-reduce(f32[32,1]{0,1:T(1,128)S(1)} %get-tuple-element.21, f32[32,1]{0,1:T(1,128)S(1)} %get-tuple-element.22), channel_id=1, replica_groups=mesh['row_0'=8,'row_1'=2,'col_0'=4,'col_1'=4] {'col_1'}, use_global_device_ids=true, to_apply=%region_30.0 | all-reduce | flops 64 | bytes 512 | tf_op jit(solution)/shard_map/psum | solution.py:40
  (38 shorter events, 11.4 us)
Async XLA Ops:
  0.6 55.2 %copy-start.2 = (f32[32,512]{1,0:T(8,128)S(1)}, f32[32,512]{1,0:T(8,128)}, u32[]{:S(2)}) copy-start(f32[32,512]{1,0:T(8,128)} %param.7) | copy-start | bytes 196612
  32.0 50.6 %copy-start = (f32[32,256]{1,0:T(8,128)S(1)}, f32[32,256]{1,0:T(8,128)}, u32[]{:S(2)}) copy-start(f32[32,256]{1,0:T(8,128)} %param.8) | copy-start | bytes 98308
  32.0 50.6 %copy-start.1 = (f32[32,256]{1,0:T(8,128)S(1)}, f32[32,256]{1,0:T(8,128)}, u32[]{:S(2)}) copy-start(f32[32,256]{1,0:T(8,128)} %param.10) | copy-start | bytes 98308
  32.0 50.6 %copy-start.3 = (f32[32,256]{1,0:T(8,128)S(1)}, f32[32,256]{1,0:T(8,128)}, u32[]{:S(2)}) copy-start(f32[32,256]{1,0:T(8,128)} %param.9) | copy-start | bytes 98308
  110.8 21.6 %all-to-all-start.2 = ((f32[16,32,512]{2,1,0:T(8,128)}), f32[16,32,512]{2,1,0:T(8,128)S(1)}, u32[]{:S(2)}, u32[]{:S(2)}) async-start(f32[16,32,512]{2,1,0:T(8,128)} %broadcast_in_dim.22), calls=%async_computation.2 | async-start | bytes 2097152 | tf_op jit(solution)/shard_map/all_to_all | solution.py:17
  339.6 36.3 %copy-start.4 = (f32[32]{0:T(128)S(1)}, f32[32]{0:T(128)}, u32[]{:S(2)}) copy-start(f32[32]{0:T(128)} %param.11) | copy-start | bytes 388
  370.5 21.3 %all-to-all-start.7 = ((f32[16,32,256]{2,1,0:T(8,128)}), f32[16,32,256]{2,1,0:T(8,128)S(1)}, u32[]{:S(2)}, u32[]{:S(2)}) async-start(f32[16,32,256]{2,1,0:T(8,128)} %convolution_bitcast_fusion), calls=%async_computation.7 | async-start | bytes 1048576 | tf_op jit(solution)/shard_map/all_to_all | solution.py:34
where the time goes:
time: 429 us; the launch traced here: 428 us
  blocking collectives  304 us (71%)
  matrix products  76.5 us (18%)
  waiting for transfers between devices  23.6 us (6%)
  local copies, waits for them, and re-layouts  10.6 us (2%)
  starting transfers between devices  10.2 us (2%)
    psum x12, blocking collectives, by_axis(): array = lax.psum(array, axis)  107 us
    all_gather x4, blocking collectives, spread(): lax.all_gather(vector, ROW, axis=1, tiled=True)  72.8 us
    all_to_all x3, blocking collectives, sent_to_all(): lax.all_to_all(jnp.broadcast_to(array[None], (peers, *array.shape)), axis...  63.4 us
    all_to_all x3, blocking collectives, summed_on_arrival(): tiles = lax.all_to_all(split_up(array, dim, peers), axis, 0, 0, tiled=True)  61.4 us
    dot_general x4, matrix products, forward_part(): lax.dot_general(vector, block, (((1,), (1,)), ((), ())), precision=lax.Pr...  38.9 us
    dot_general x4, matrix products, backward_part(): jnp.dot(values, design, precision=lax.Precision.HIGHEST, preferred_elemen...  37.6 us
    all_to_all x1, waiting for transfers between devices, summed_on_arrival(): tiles = lax.all_to_all(split_up(array, dim, peers), axis, 0, 0, tiled=True)  15.9 us
    dot_general x1, local copies, waits for them, and re-layouts, backward_part(): jnp.dot(values, design, precision=lax.Precision.HIGHEST, preferred_elemen...  9.01 us
  transfers between devices with their start and end apart: 2, of which 2 were waited for; matrix products, arithmetic and copies ran while one was open for 2% of the time, Pallas kernels for 0%

commit v1 on v0

--- a/solution.py
+++ b/solution.py
@@ -67,7 +67,13 @@
         return taken_together(partial_value, COL)
 
     def spread(vector):
-        return rows_total(forward_part(lax.all_gather(vector, ROW, axis=1, tiled=True), design))
+
+        def name_forms(packet):
+            return jnp.concatenate(
+                lax.all_to_all(jnp.stack(lax.axis_size(ROW) * [packet], 0), ROW, 0, 0), 1
+            )
+
+        return rows_total(forward_part(name_forms(vector), design))
 
     def collect(values):
         return summed_on_arrival(backward_part(values, design), ROW, 1)

time: 429 us -> 443 us (1.033)
  blocking collectives: 304 us -> 318 us
    all_to_all x0 -> x4, blocking collectives: none -> 87.9 us  [name_forms(): lax.all_to_all(jnp.stack(lax.axis_size(ROW) * [packet], 0), ROW, 0, 0)]
    all_gather x4 -> x0, blocking collectives: 72.8 us -> none  [spread(): lax.all_gather(vector, ROW, axis=1, tiled=True)]
where the time goes in v1:
time: 443 us; the launch traced here: 442 us
  blocking collectives  318 us (72%)
  matrix products  76.5 us (17%)
  waiting for transfers between devices  23.4 us (5%)
  local copies, waits for them, and re-layouts  11.7 us (3%)
  starting transfers between devices  8.48 us (2%)
    psum x12, blocking collectives, by_axis(): array = lax.psum(array, axis)  107 us
    all_to_all x4, blocking collectives, name_forms(): lax.all_to_all(jnp.stack(lax.axis_size(ROW) * [packet], 0), ROW, 0, 0)  87.9 us
    all_to_all x3, blocking collectives, sent_to_all(): lax.all_to_all(jnp.broadcast_to(array[None], (peers, *array.shape)), axis...  64.8 us
    all_to_all x3, blocking collectives, summed_on_arrival(): tiles = lax.all_to_all(split_up(array, dim, peers), axis, 0, 0, tiled=True)  58.3 us
    dot_general x4, matrix products, forward_part(): lax.dot_general(vector, block, (((1,), (1,)), ((), ())), precision=lax.Pr...  38.9 us
    dot_general x4, matrix products, backward_part(): jnp.dot(values, design, precision=lax.Precision.HIGHEST, preferred_elemen...  37.6 us
    all_to_all x1, waiting for transfers between devices, summed_on_arrival(): tiles = lax.all_to_all(split_up(array, dim, peers), axis, 0, 0, tiled=True)  15.9 us
    dot_general x1, local copies, waits for them, and re-layouts, backward_part(): jnp.dot(values, design, precision=lax.Precision.HIGHEST, preferred_elemen...  9.01 us
  transfers between devices with their start and end apart: 2, of which 2 were waited for; matrix products, arithmetic and copies ran while one was open for 2% of the time, Pallas kernels for 0%

profile of v1, /device:TPU:2, one launch (start us, length us, event | category | flops | bytes accessed | tf_op | source)
XLA Modules:
  0.0 441.6 jit_solution(17682828404812773208)
XLA Ops:
  1.5 24.3 %all_to_all.60 = f32[16,32,256]{2,1,0:T(8,128)S(1)} all-to-all(f32[16,32,256]{2,1,0:T(8,128)S(1)} %stack.8), channel_id=1, replica_groups=mesh['row_0'=8,'row_1'=2,'col_0'=4,'col_1'=4] {'row_0','row_1'}, dimensions={0} | all-to-all | bytes 1048576 | tf_op jit(solution)/shard_map/all_to_all | solution.py:73
  25.8 9.7 %fusion.8 = f32[32,512]{1,0:T(8,128)S(1)} fusion(f32[32,4096]{1,0:T(8,128)S(1)} %bitcast.66, f32[512,4096]{1,0:T(8,128)} %param.6), kind=kOutput, calls=%fused_computation.30 | convolution fusion | flops 805306368 | bytes 8978432 | tf_op jit(solution)/shard_map/dot_general | solution.py:45
  35.7 24.1 %all_to_all.61 = f32[16,32,512]{2,1,0:T(8,128)S(1)} all-to-all(f32[16,32,512]{2,1,0:T(8,128)S(1)} %broadcast_in_dim.20), channel_id=1, replica_groups=mesh['row_0'=8,'row_1'=2,'col_0'=4,'col_1'=4] {'col_0','col_1'}, dimensions={0} | all-to-all | bytes 2097152 | tf_op jit(solution)/shard_map/all_to_all | solution.py:17
  59.9 7.2 %fusion.3 = f32[32,4096]{1,0:T(8,128)S(1)} fusion(f32[512,4096]{1,0:T(8,128)} %param.6, f32[32,512]{1,0:T(8,128)S(1)} %copy-done.2, f32[32,512]{1,0:T(8,128)S(1)} %reduce_sum.126), kind=kOutput, calls=%fused_computation.7 | convolution fusion | flops 805322752 | bytes 9043968 | tf_op jit(solution)/shard_map/dot_general | solution.py:55
  67.1 19.2 %all_to_all.62 = f32[16,32,256]{2,1,0:T(8,128)S(1)} all-to-all(f32[16,32,256]{2,1,0:T(8,128)S(1)} %bitcast.72), channel_id=1, replica_groups=mesh['row_0'=8,'row_1'=2,'col_0'=4,'col_1'=4] {'row_0','row_1'}, dimensions={0} | all-to-all | bytes 1048576 | tf_op jit(solution)/shard_map/all_to_all | solution.py:34
  86.5 20.0 %all_to_all.63 = f32[16,32,256]{2,1,0:T(8,128)S(1)} all-to-all(f32[16,32,256]{2,1,0:T(8,128)S(1)} %stack.9), channel_id=1, replica_groups=mesh['row_0'=8,'row_1'=2,'col_0'=4,'col_1'=4] {'row_0','row_1'}, dimensions={0} | all-to-all | bytes 1048576 | tf_op jit(solution)/shard_map/all_to_all | solution.py:73
  106.5 9.7 %fusion.9 = f32[32,512]{1,0:T(8,128)S(1)} fusion(f32[32,4096]{1,0:T(8,128)S(1)} %bitcast.68, f32[512,4096]{1,0:T(8,128)} %param.6), kind=kOutput, calls=%fused_computation.31 | convolution fusion | flops 805306368 | bytes 8978432 | tf_op jit(solution)/shard_map/dot_general | solution.py:45
  117.5 4.9 %all-to-all-start.4 = ((f32[16,32,512]{2,1,0:T(8,128)}), f32[16,32,512]{2,1,0:T(8,128)S(1)}, u32[]{:S(2)}, u32[]{:S(2)}) async-start(f32[16,32,512]{2,1,0:T(8,128)} %broadcast_in_dim.22), calls=%async_computation.4 | async-start | bytes 2097152 | tf_op jit(solution)/shard_map/all_to_all | solution.py:17
  122.4 9.0 %copy.31 = f32[4096,512]{1,0:T(8,128)} copy(f32[4096,512]{0,1:T(8,128)} %bitcast.62) | data formatting | bytes 16777216 | tf_op jit(solution)/shard_map/dot_general | solution.py:55
  131.4 7.6 %all-to-all-done.4 = f32[16,32,512]{2,1,0:T(8,128)S(1)} async-done(((f32[16,32,512]{2,1,0:T(8,128)}), f32[16,32,512]{2,1,0:T(8,128)S(1)}, u32[]{:S(2)}, u32[]{:S(2)}) %all-to-all-start.4) | async-done | bytes 1048608 | tf_op jit(solution)/shard_map/all_to_all | solution.py:17
  139.0 9.9 %convolution_bitcast_fusion.2 = f32[16,32,256]{2,1,0:T(8,128)S(1)} fusion(f32[16,256,512]{2,1,0:T(8,128)} %bitcast.63, f32[32,512]{1,0:T(8,128)S(1)} %reduce_sum.129), kind=kOutput, calls=%fused_computation.2 | convolution fusion | flops 805306368 | bytes 8978432 | tf_op jit(solution)/shard_map/dot_general | solution.py:55
  148.9 19.8 %all_to_all.64 = f32[16,32,256]{2,1,0:T(8,128)S(1)} all-to-all(f32[16,32,256]{2,1,0:T(8,128)S(1)} %convolution_bitcast_fusion.2), channel_id=1, replica_groups=mesh['row_0'=8,'row_1'=2,'col_0'=4,'col_1'=4] {'row_0','row_1'}, dimensions={0} | all-to-all | bytes 1048576 | tf_op jit(solution)/shard_map/all_to_all | solution.py:34
  168.9 14.9 %all-reduce.2 = (f32[32,1]{0,1:T(1,128)S(1)}, f32[32,1]{0,1:T(1,128)S(1)}) all-reduce(f32[32,1]{0,1:T(1,128)S(1)} %bitcast.82, f32[32,1]{0,1:T(1,128)S(1)} %bitcast.81), channel_id=1, replica_groups=mesh['row_0'=8,'row_1'=2,'col_0'=4,'col_1'=4] {'row_0'}, use_global_device_ids=true, to_apply=%region_3.0 | all-reduce | flops 64 | bytes 512 | tf_op jit(solution)/shard_map/psum | solution.py:40
  186.3 8.7 %all-reduce.8 = (f32[32,1]{0,1:T(1,128)S(1)}, f32[32,1]{0,1:T(1,128)S(1)}) all-reduce(f32[32,1]{0,1:T(1,128)S(1)} %get-tuple-element.31, f32[32,1]{0,1:T(1,128)S(1)} %get-tuple-element.32), channel_id=1, replica_groups=mesh['row_0'=8,'row_1'=2,'col_0'=4,'col_1'=4] {'col_0'}, use_global_device_ids=true, to_apply=%region_5.0 | all-reduce | flops 64 | bytes 512 | tf_op jit(solution)/shard_map/psum | solution.py:40
  194.9 10.8 %all-reduce.5 = (f32[32,1]{0,1:T(1,128)S(1)}, f32[32,1]{0,1:T(1,128)S(1)}) all-reduce(f32[32,1]{0,1:T(1,128)S(1)} %get-tuple-element.25, f32[32,1]{0,1:T(1,128)S(1)} %get-tuple-element.26), channel_id=1, replica_groups=mesh['row_0'=8,'row_1'=2,'col_0'=4,'col_1'=4] {'col_1'}, use_global_device_ids=true, to_apply=%region_6.0 | all-reduce | flops 64 | bytes 512 | tf_op jit(solution)/shard_map/psum | solution.py:40
  205.8 21.8 %all_to_all.65 = f32[16,32,256]{2,1,0:T(8,128)S(1)} all-to-all(f32[16,32,256]{2,1,0:T(8,128)S(1)} %stack.10), channel_id=1, replica_groups=mesh['row_0'=8,'row_1'=2,'col_0'=4,'col_1'=4] {'row_0','row_1'}, dimensions={0} | all-to-all | bytes 1048576 | tf_op jit(solution)/shard_map/all_to_all | solution.py:73
  227.7 9.7 %fusion.10 = f32[32,512]{1,0:T(8,128)S(1)} fusion(f32[32,4096]{1,0:T(8,128)S(1)} %bitcast.69, f32[512,4096]{1,0:T(8,128)} %param.6), kind=kOutput, calls=%fused_computation.32 | convolution fusion | flops 805306368 | bytes 8978432 | tf_op jit(solution)/shard_map/dot_general | solution.py:45
  237.6 20.2 %all_to_all.66 = f32[16,32,512]{2,1,0:T(8,128)S(1)} all-to-all(f32[16,32,512]{2,1,0:T(8,128)S(1)} %broadcast_in_dim.48), channel_id=1, replica_groups=mesh['row_0'=8,'row_1'=2,'col_0'=4,'col_1'=4] {'col_0','col_1'}, dimensions={0} | all-to-all | bytes 2097152 | tf_op jit(solution)/shard_map/all_to_all | solution.py:17
  257.8 9.9 %convolution_bitcast_fusion.1 = f32[16,32,256]{2,1,0:T(8,128)S(1)} fusion(f32[16,256,512]{2,1,0:T(8,128)} %bitcast.64, f32[32,512]{1,0:T(8,128)S(1)} %reduce_sum.133), kind=kOutput, calls=%fused_computation.1 | convolution fusion | flops 805306368 | bytes 8978432 | tf_op jit(solution)/shard_map/dot_general | solution.py:55
  267.7 19.2 %all_to_all.67 = f32[16,32,256]{2,1,0:T(8,128)S(1)} all-to-all(f32[16,32,256]{2,1,0:T(8,128)S(1)} %convolution_bitcast_fusion.1), channel_id=1, replica_groups=mesh['row_0'=8,'row_1'=2,'col_0'=4,'col_1'=4] {'row_0','row_1'}, dimensions={0} | all-to-all | bytes 1048576 | tf_op jit(solution)/shard_map/all_to_all | solution.py:34
  287.1 14.9 %all-reduce.1 = (f32[32,1]{0,1:T(1,128)S(1)}, f32[32,1]{0,1:T(1,128)S(1)}) all-reduce(f32[32,1]{0,1:T(1,128)S(1)} %bitcast.84, f32[32,1]{0,1:T(1,128)S(1)} %bitcast.83), channel_id=1, replica_groups=mesh['row_0'=8,'row_1'=2,'col_0'=4,'col_1'=4] {'row_0'}, use_global_device_ids=true, to_apply=%region_15.0 | all-reduce | flops 64 | bytes 512 | tf_op jit(solution)/shard_map/psum | solution.py:40
  304.5 8.6 %all-reduce.7 = (f32[32,1]{0,1:T(1,128)S(1)}, f32[32,1]{0,1:T(1,128)S(1)}) all-reduce(f32[32,1]{0,1:T(1,128)S(1)} %get-tuple-element.29, f32[32,1]{0,1:T(1,128)S(1)} %get-tuple-element.30), channel_id=1, replica_groups=mesh['row_0'=8,'row_1'=2,'col_0'=4,'col_1'=4] {'col_0'}, use_global_device_ids=true, to_apply=%region_17.0 | all-reduce | flops 64 | bytes 512 | tf_op jit(solution)/shard_map/psum | solution.py:40
  313.0 9.2 %all-reduce.4 = (f32[32,1]{0,1:T(1,128)S(1)}, f32[32,1]{0,1:T(1,128)S(1)}) all-reduce(f32[32,1]{0,1:T(1,128)S(1)} %get-tuple-element.23, f32[32,1]{0,1:T(1,128)S(1)} %get-tuple-element.24), channel_id=1, replica_groups=mesh['row_0'=8,'row_1'=2,'col_0'=4,'col_1'=4] {'col_1'}, use_global_device_ids=true, to_apply=%region_18.0 | all-reduce | flops 64 | bytes 512 | tf_op jit(solution)/shard_map/psum | solution.py:40
  322.4 21.8 %all_to_all.68 = f32[16,32,256]{2,1,0:T(8,128)S(1)} all-to-all(f32[16,32,256]{2,1,0:T(8,128)S(1)} %stack.11), channel_id=1, replica_groups=mesh['row_0'=8,'row_1'=2,'col_0'=4,'col_1'=4] {'row_0','row_1'}, dimensions={0} | all-to-all | bytes 1048576 | tf_op jit(solution)/shard_map/all_to_all | solution.py:73
  344.2 9.7 %fusion.11 = f32[32,512]{1,0:T(8,128)S(1)} fusion(f32[32,4096]{1,0:T(8,128)S(1)} %bitcast.70, f32[512,4096]{1,0:T(8,128)} %param.6), kind=kOutput, calls=%fused_computation.33 | convolution fusion | flops 805306368 | bytes 8978432 | tf_op jit(solution)/shard_map/dot_general | solution.py:45
  354.1 20.5 %all_to_all.69 = f32[16,32,512]{2,1,0:T(8,128)S(1)} all-to-all(f32[16,32,512]{2,1,0:T(8,128)S(1)} %broadcast_in_dim.51), channel_id=1, replica_groups=mesh['row_0'=8,'row_1'=2,'col_0'=4,'col_1'=4] {'col_0','col_1'}, dimensions={0} | all-to-all | bytes 2097152 | tf_op jit(solution)/shard_map/all_to_all | solution.py:17
  374.7 10.7 %convolution_bitcast_fusion = f32[16,32,256]{2,1,0:T(8,128)} fusion(f32[16,256,512]{2,1,0:T(8,128)} %bitcast.65, f32[32,512]{1,0:T(8,128)S(1)} %reduce_sum.137), kind=kOutput, calls=%fused_computation | convolution fusion | flops 805306368 | bytes 8978432 | tf_op jit(solution)/shard_map/dot_general | solution.py:55
  385.4 3.6 all-to-all-start.11
  389.0 15.9 %all-to-all-done.11 = f32[16,32,256]{2,1,0:T(8,128)S(1)} async-done(((f32[16,32,256]{2,1,0:T(8,128)}), f32[16,32,256]{2,1,0:T(8,128)S(1)}, u32[]{:S(2)}, u32[]{:S(2)}) %all-to-all-start.11) | async-done | bytes 524320 | tf_op jit(solution)/shard_map/all_to_all | solution.py:34
  405.0 15.0 %all-reduce = (f32[32,1]{0,1:T(1,128)S(1)}, f32[32,1]{0,1:T(1,128)S(1)}) all-reduce(f32[32,1]{0,1:T(1,128)S(1)} %bitcast.80, f32[32,1]{0,1:T(1,128)S(1)} %bitcast.79), channel_id=1, replica_groups=mesh['row_0'=8,'row_1'=2,'col_0'=4,'col_1'=4] {'row_0'}, use_global_device_ids=true, to_apply=%region_27.0 | all-reduce | flops 64 | bytes 512 | tf_op jit(solution)/shard_map/psum | solution.py:40
  422.4 8.6 %all-reduce.6 = (f32[32,1]{0,1:T(1,128)S(1)}, f32[32,1]{0,1:T(1,128)S(1)}) all-reduce(f32[32,1]{0,1:T(1,128)S(1)} %get-tuple-element.27, f32[32,1]{0,1:T(1,128)S(1)} %get-tuple-element.28), channel_id=1, replica_groups=mesh['row_0'=8,'row_1'=2,'col_0'=4,'col_1'=4] {'col_0'}, use_global_device_ids=true, to_apply=%region_29.0 | all-reduce | flops 64 | bytes 512 | tf_op jit(solution)/shard_map/psum | solution.py:40
  431.0 9.2 %all-reduce.3 = (f32[32,1]{0,1:T(1,128)S(1)}, f32[32,1]{0,1:T(1,128)S(1)}) all-reduce(f32[32,1]{0,1:T(1,128)S(1)} %get-tuple-element.21, f32[32,1]{0,1:T(1,128)S(1)} %get-tuple-element.22), channel_id=1, replica_groups=mesh['row_0'=8,'row_1'=2,'col_0'=4,'col_1'=4] {'col_1'}, use_global_device_ids=true, to_apply=%region_30.0 | all-reduce | flops 64 | bytes 512 | tf_op jit(solution)/shard_map/psum | solution.py:40
  (46 shorter events, 12.5 us)
Async XLA Ops:
  0.6 59.3 %copy-start.2 = (f32[32,512]{1,0:T(8,128)S(1)}, f32[32,512]{1,0:T(8,128)}, u32[]{:S(2)}) copy-start(f32[32,512]{1,0:T(8,128)} %param.7) | copy-start | bytes 196612
  35.6 50.8 %copy-start = (f32[32,256]{1,0:T(8,128)S(1)}, f32[32,256]{1,0:T(8,128)}, u32[]{:S(2)}) copy-start(f32[32,256]{1,0:T(8,128)} %param.8) | copy-start | bytes 98308
  35.6 50.8 %copy-start.1 = (f32[32,256]{1,0:T(8,128)S(1)}, f32[32,256]{1,0:T(8,128)}, u32[]{:S(2)}) copy-start(f32[32,256]{1,0:T(8,128)} %param.10) | copy-start | bytes 98308
  35.6 50.8 %copy-start.3 = (f32[32,256]{1,0:T(8,128)S(1)}, f32[32,256]{1,0:T(8,128)}, u32[]{:S(2)}) copy-start(f32[32,256]{1,0:T(8,128)} %param.9) | copy-start | bytes 98308
  117.5 21.5 %all-to-all-start.4 = ((f32[16,32,512]{2,1,0:T(8,128)}), f32[16,32,512]{2,1,0:T(8,128)S(1)}, u32[]{:S(2)}, u32[]{:S(2)}) async-start(f32[16,32,512]{2,1,0:T(8,128)} %broadcast_in_dim.22), calls=%async_computation.4 | async-start | bytes 2097152 | tf_op jit(solution)/shard_map/all_to_all | solution.py:17
  354.0 35.0 %copy-start.4 = (f32[32]{0:T(128)S(1)}, f32[32]{0:T(128)}, u32[]{:S(2)}) copy-start(f32[32]{0:T(128)} %param.11) | copy-start | bytes 388
  385.4 19.5 %all-to-all-start.11 = ((f32[16,32,256]{2,1,0:T(8,128)}), f32[16,32,256]{2,1,0:T(8,128)S(1)}, u32[]{:S(2)}, u32[]{:S(2)}) async-start(f32[16,32,256]{2,1,0:T(8,128)} %convolution_bitcast_fusion), calls=%async_computation.11 | async-start | bytes 1048576 | tf_op jit(solution)/shard_map/all_to_all | solution.py:34
